TPU v7x, 32 devices: a 4x4x1 block of a 4x4x8 slice. The times are simulated.
32 devices in a mesh: dp: 1 (over z), cp: 32 (over y, x, core).
Axes of the slice: x: 4, y: 4, z: 1, core: 2. Of those that a mesh axis runs over, the one named last changes fastest.
The devices are a block of a 4x4x8 slice.
Arguments:
- queries: bfloat16 [768, 40, 128], P(('dp', 'cp'))
- key_new: bfloat16 [768, 8, 128], P(('dp', 'cp'))
- value_new: bfloat16 [768, 8, 128], P(('dp', 'cp'))
- key_cache: bfloat16 [32768, 8, 128], P(('dp', 'cp'))
- value_cache: bfloat16 [32768, 8, 128], P(('dp', 'cp'))
- prefix_len: int32 [1], P('dp')
Outputs:
- output 1: bfloat16 [768, 40, 128], P(('dp', 'cp'))
- output 2: float32 [768, 40], P(('dp', 'cp'))
All inputs are finite; a program needn't handle non-finite values.
Results may differ from a plain program's by a relative error of at most 0.00908133.
Values are sent between devices in bfloat16 or wider.
A program may use at most 768 MiB of HBM per device.

v0:
```python
import jax
import jax.numpy as jnp
from jax import lax
from jax.sharding import PartitionSpec as P

MASK_FILL = -1e30


def solution(mesh):
    groups = mesh.shape['cp']
    send_pairs = [(src_idx, (src_idx + 1) % groups) for src_idx in range(groups)]
    tok_spec = P(('dp', 'cp'))

    def local_attend(queries, key_new, value_new, key_cache, value_cache, prefix_len):
        tok_rows, num_heads, head_dim = queries.shape
        cache_len, kv_heads = key_cache.shape[0], key_cache.shape[1]
        group_ratio = num_heads // kv_heads
        logit_scale = head_dim ** -0.5
        my_rank = lax.axis_index('cp')
        cache_seen = my_rank * cache_len + jnp.arange(cache_len) < prefix_len[0]
        row_ids = jnp.arange(tok_rows)
        key_ids = my_rank * tok_rows + row_ids

        def absorb(loop_step, q_blk, out_acc, row_max, row_sum):
            source = (my_rank - loop_step) % groups
            q_grouped = q_blk.reshape(tok_rows, kv_heads, group_ratio, head_dim)
            s_cache = jnp.einsum('tkgd,skd->kgts', q_grouped, key_cache, preferred_element_type=jnp.float32) * logit_scale
            s_cache = jnp.where(cache_seen, s_cache, MASK_FILL)
            s_fresh = jnp.einsum('tkgd,skd->kgts', q_grouped, key_new, preferred_element_type=jnp.float32) * logit_scale
            fresh_seen = key_ids[None, :] <= (source * tok_rows + row_ids)[:, None]
            s_fresh = jnp.where(fresh_seen, s_fresh, MASK_FILL)
            next_max = jnp.maximum(row_max, jnp.maximum(s_cache.max(axis=-1), s_fresh.max(axis=-1)))
            e_cache = jnp.exp(s_cache - next_max[..., None])
            e_fresh = jnp.exp(s_fresh - next_max[..., None])
            rescale_by = jnp.exp(row_max - next_max)
            row_sum = row_sum * rescale_by + e_cache.sum(axis=-1) + e_fresh.sum(axis=-1)
            out_acc = (out_acc * rescale_by[..., None]
                       + jnp.einsum('kgts,skd->kgtd', e_cache.astype(jnp.bfloat16), value_cache, preferred_element_type=jnp.float32)
                       + jnp.einsum('kgts,skd->kgtd', e_fresh.astype(jnp.bfloat16), value_new, preferred_element_type=jnp.float32))
            return out_acc, next_max, row_sum

        def one_step(loop_step, state):
            q_blk, out_acc, row_max, row_sum = state
            out_acc, row_max, row_sum = absorb(loop_step, q_blk, out_acc, row_max, row_sum)
            return lax.ppermute((q_blk, out_acc, row_max, row_sum), 'cp', send_pairs)

        start_acc = jnp.zeros((kv_heads, group_ratio, tok_rows, head_dim), jnp.float32)
        start_max = jnp.full((kv_heads, group_ratio, tok_rows), MASK_FILL, jnp.float32)
        start_sum = jnp.zeros((kv_heads, group_ratio, tok_rows), jnp.float32)
        q_blk, out_acc, row_max, row_sum = lax.fori_loop(0, groups - 1, one_step, (queries, start_acc, start_max, start_sum))
        out_acc, row_max, row_sum = absorb(groups - 1, q_blk, out_acc, row_max, row_sum)
        out_acc, row_max, row_sum = lax.ppermute((out_acc, row_max, row_sum), 'cp', send_pairs)
        attn_out = (out_acc / row_sum[..., None]).transpose(2, 0, 1, 3).reshape(tok_rows, num_heads, head_dim).astype(jnp.bfloat16)
        row_lse = (row_max + jnp.log(row_sum)).transpose(2, 0, 1).reshape(tok_rows, num_heads)
        return attn_out, row_lse

    return jax.shard_map(local_attend, mesh=mesh, in_specs=(tok_spec, tok_spec, tok_spec, tok_spec, tok_spec, P('dp')), out_specs=(tok_spec, tok_spec), check_vma=False)
```

profile of v0, /device:TPU:96, one launch (start us, length us, event | category | flops | bytes accessed | tf_op | source)
XLA Modules:
  0.0 705.5 jit_solution(1509250502634326383)
XLA Ops:
  7.0 676.7 %while.22 = (s32[]{:T(128)}, bf16[24,40,128]{2,0,1:T(8,128)(2,1)S(1)}, f32[8,5,24,128]{3,2,1,0:T(8,128)}, f32[8,5,24]{2,1,0:T(8,128)S(1)}, f32[8,5,24]{2,1,0:T(8...) while((s32[]{:T(128)}, ...), condition=%wide.region_5.6_spmd.clone, body=%wide.region_0.5_spmd.clone.sunk | while | flops 526460928 | bytes 30766068 | solution.py:50
  16.8 12.8 %collective-permute-done.2 = f32[8,5,24]{2,1,0:T(8,128)S(1)} collective-permute-done((f32[8,5,24]{2,1,0:T(8,128)S(1)}, f32[8,5,24]{2,1,0:T(8,128)S(1)}, u32[]{:S(2)}, u32[]{:S(2)}) %collective-permute-start.2) | collective-permute-done | bytes 3872 | tf_op jit(solution)/shard_map/while/body/eval_jaxpr/ppermute | solution.py:45
  33.9 2.5 fusion.85
  37.2 14.2 %collective-permute-done.2 = f32[8,5,24]{2,1,0:T(8,128)S(1)} collective-permute-done((f32[8,5,24]{2,1,0:T(8,128)S(1)}, f32[8,5,24]{2,1,0:T(8,128)S(1)}, u32[]{:S(2)}, u32[]{:S(2)}) %collective-permute-start.2) | collective-permute-done | bytes 3872 | tf_op jit(solution)/shard_map/while/body/eval_jaxpr/ppermute | solution.py:45
  55.7 2.5 fusion.85
  59.0 14.2 %collective-permute-done.2 = f32[8,5,24]{2,1,0:T(8,128)S(1)} collective-permute-done((f32[8,5,24]{2,1,0:T(8,128)S(1)}, f32[8,5,24]{2,1,0:T(8,128)S(1)}, u32[]{:S(2)}, u32[]{:S(2)}) %collective-permute-start.2) | collective-permute-done | bytes 3872 | tf_op jit(solution)/shard_map/while/body/eval_jaxpr/ppermute | solution.py:45
  77.5 2.5 fusion.85
  80.8 14.2 %collective-permute-done.2 = f32[8,5,24]{2,1,0:T(8,128)S(1)} collective-permute-done((f32[8,5,24]{2,1,0:T(8,128)S(1)}, f32[8,5,24]{2,1,0:T(8,128)S(1)}, u32[]{:S(2)}, u32[]{:S(2)}) %collective-permute-start.2) | collective-permute-done | bytes 3872 | tf_op jit(solution)/shard_map/while/body/eval_jaxpr/ppermute | solution.py:45
  99.3 2.5 fusion.85
  102.6 14.2 %collective-permute-done.2 = f32[8,5,24]{2,1,0:T(8,128)S(1)} collective-permute-done((f32[8,5,24]{2,1,0:T(8,128)S(1)}, f32[8,5,24]{2,1,0:T(8,128)S(1)}, u32[]{:S(2)}, u32[]{:S(2)}) %collective-permute-start.2) | collective-permute-done | bytes 3872 | tf_op jit(solution)/shard_map/while/body/eval_jaxpr/ppermute | solution.py:45
  121.1 2.5 fusion.85
  124.3 14.2 %collective-permute-done.2 = f32[8,5,24]{2,1,0:T(8,128)S(1)} collective-permute-done((f32[8,5,24]{2,1,0:T(8,128)S(1)}, f32[8,5,24]{2,1,0:T(8,128)S(1)}, u32[]{:S(2)}, u32[]{:S(2)}) %collective-permute-start.2) | collective-permute-done | bytes 3872 | tf_op jit(solution)/shard_map/while/body/eval_jaxpr/ppermute | solution.py:45
  142.9 2.5 fusion.85
  146.1 14.2 %collective-permute-done.2 = f32[8,5,24]{2,1,0:T(8,128)S(1)} collective-permute-done((f32[8,5,24]{2,1,0:T(8,128)S(1)}, f32[8,5,24]{2,1,0:T(8,128)S(1)}, u32[]{:S(2)}, u32[]{:S(2)}) %collective-permute-start.2) | collective-permute-done | bytes 3872 | tf_op jit(solution)/shard_map/while/body/eval_jaxpr/ppermute | solution.py:45
  164.7 2.5 fusion.85
  167.9 14.2 %collective-permute-done.2 = f32[8,5,24]{2,1,0:T(8,128)S(1)} collective-permute-done((f32[8,5,24]{2,1,0:T(8,128)S(1)}, f32[8,5,24]{2,1,0:T(8,128)S(1)}, u32[]{:S(2)}, u32[]{:S(2)}) %collective-permute-start.2) | collective-permute-done | bytes 3872 | tf_op jit(solution)/shard_map/while/body/eval_jaxpr/ppermute | solution.py:45
  186.5 2.5 fusion.85
  189.7 14.2 %collective-permute-done.2 = f32[8,5,24]{2,1,0:T(8,128)S(1)} collective-permute-done((f32[8,5,24]{2,1,0:T(8,128)S(1)}, f32[8,5,24]{2,1,0:T(8,128)S(1)}, u32[]{:S(2)}, u32[]{:S(2)}) %collective-permute-start.2) | collective-permute-done | bytes 3872 | tf_op jit(solution)/shard_map/while/body/eval_jaxpr/ppermute | solution.py:45
  208.2 2.5 fusion.85
  211.5 14.2 %collective-permute-done.2 = f32[8,5,24]{2,1,0:T(8,128)S(1)} collective-permute-done((f32[8,5,24]{2,1,0:T(8,128)S(1)}, f32[8,5,24]{2,1,0:T(8,128)S(1)}, u32[]{:S(2)}, u32[]{:S(2)}) %collective-permute-start.2) | collective-permute-done | bytes 3872 | tf_op jit(solution)/shard_map/while/body/eval_jaxpr/ppermute | solution.py:45
  230.0 2.5 fusion.85
  233.3 14.2 %collective-permute-done.2 = f32[8,5,24]{2,1,0:T(8,128)S(1)} collective-permute-done((f32[8,5,24]{2,1,0:T(8,128)S(1)}, f32[8,5,24]{2,1,0:T(8,128)S(1)}, u32[]{:S(2)}, u32[]{:S(2)}) %collective-permute-start.2) | collective-permute-done | bytes 3872 | tf_op jit(solution)/shard_map/while/body/eval_jaxpr/ppermute | solution.py:45
  251.8 2.5 fusion.85
  255.1 14.2 %collective-permute-done.2 = f32[8,5,24]{2,1,0:T(8,128)S(1)} collective-permute-done((f32[8,5,24]{2,1,0:T(8,128)S(1)}, f32[8,5,24]{2,1,0:T(8,128)S(1)}, u32[]{:S(2)}, u32[]{:S(2)}) %collective-permute-start.2) | collective-permute-done | bytes 3872 | tf_op jit(solution)/shard_map/while/body/eval_jaxpr/ppermute | solution.py:45
  273.6 2.5 fusion.85
  276.9 14.2 %collective-permute-done.2 = f32[8,5,24]{2,1,0:T(8,128)S(1)} collective-permute-done((f32[8,5,24]{2,1,0:T(8,128)S(1)}, f32[8,5,24]{2,1,0:T(8,128)S(1)}, u32[]{:S(2)}, u32[]{:S(2)}) %collective-permute-start.2) | collective-permute-done | bytes 3872 | tf_op jit(solution)/shard_map/while/body/eval_jaxpr/ppermute | solution.py:45
  295.4 2.5 fusion.85
  298.7 14.2 %collective-permute-done.2 = f32[8,5,24]{2,1,0:T(8,128)S(1)} collective-permute-done((f32[8,5,24]{2,1,0:T(8,128)S(1)}, f32[8,5,24]{2,1,0:T(8,128)S(1)}, u32[]{:S(2)}, u32[]{:S(2)}) %collective-permute-start.2) | collective-permute-done | bytes 3872 | tf_op jit(solution)/shard_map/while/body/eval_jaxpr/ppermute | solution.py:45
  317.2 2.5 fusion.85
  320.5 14.2 %collective-permute-done.2 = f32[8,5,24]{2,1,0:T(8,128)S(1)} collective-permute-done((f32[8,5,24]{2,1,0:T(8,128)S(1)}, f32[8,5,24]{2,1,0:T(8,128)S(1)}, u32[]{:S(2)}, u32[]{:S(2)}) %collective-permute-start.2) | collective-permute-done | bytes 3872 | tf_op jit(solution)/shard_map/while/body/eval_jaxpr/ppermute | solution.py:45
  339.0 2.5 fusion.85
  342.3 14.2 %collective-permute-done.2 = f32[8,5,24]{2,1,0:T(8,128)S(1)} collective-permute-done((f32[8,5,24]{2,1,0:T(8,128)S(1)}, f32[8,5,24]{2,1,0:T(8,128)S(1)}, u32[]{:S(2)}, u32[]{:S(2)}) %collective-permute-start.2) | collective-permute-done | bytes 3872 | tf_op jit(solution)/shard_map/while/body/eval_jaxpr/ppermute | solution.py:45
  360.8 2.5 fusion.85
  364.1 14.2 %collective-permute-done.2 = f32[8,5,24]{2,1,0:T(8,128)S(1)} collective-permute-done((f32[8,5,24]{2,1,0:T(8,128)S(1)}, f32[8,5,24]{2,1,0:T(8,128)S(1)}, u32[]{:S(2)}, u32[]{:S(2)}) %collective-permute-start.2) | collective-permute-done | bytes 3872 | tf_op jit(solution)/shard_map/while/body/eval_jaxpr/ppermute | solution.py:45
  382.6 2.5 fusion.85
  385.9 14.2 %collective-permute-done.2 = f32[8,5,24]{2,1,0:T(8,128)S(1)} collective-permute-done((f32[8,5,24]{2,1,0:T(8,128)S(1)}, f32[8,5,24]{2,1,0:T(8,128)S(1)}, u32[]{:S(2)}, u32[]{:S(2)}) %collective-permute-start.2) | collective-permute-done | bytes 3872 | tf_op jit(solution)/shard_map/while/body/eval_jaxpr/ppermute | solution.py:45
  404.4 2.5 fusion.85
  407.7 14.2 %collective-permute-done.2 = f32[8,5,24]{2,1,0:T(8,128)S(1)} collective-permute-done((f32[8,5,24]{2,1,0:T(8,128)S(1)}, f32[8,5,24]{2,1,0:T(8,128)S(1)}, u32[]{:S(2)}, u32[]{:S(2)}) %collective-permute-start.2) | collective-permute-done | bytes 3872 | tf_op jit(solution)/shard_map/while/body/eval_jaxpr/ppermute | solution.py:45
  426.2 2.5 fusion.85
  429.5 14.2 %collective-permute-done.2 = f32[8,5,24]{2,1,0:T(8,128)S(1)} collective-permute-done((f32[8,5,24]{2,1,0:T(8,128)S(1)}, f32[8,5,24]{2,1,0:T(8,128)S(1)}, u32[]{:S(2)}, u32[]{:S(2)}) %collective-permute-start.2) | collective-permute-done | bytes 3872 | tf_op jit(solution)/shard_map/while/body/eval_jaxpr/ppermute | solution.py:45
  448.0 2.5 fusion.85
  451.3 14.2 %collective-permute-done.2 = f32[8,5,24]{2,1,0:T(8,128)S(1)} collective-permute-done((f32[8,5,24]{2,1,0:T(8,128)S(1)}, f32[8,5,24]{2,1,0:T(8,128)S(1)}, u32[]{:S(2)}, u32[]{:S(2)}) %collective-permute-start.2) | collective-permute-done | bytes 3872 | tf_op jit(solution)/shard_map/while/body/eval_jaxpr/ppermute | solution.py:45
  469.8 2.5 fusion.85
  473.0 14.2 %collective-permute-done.2 = f32[8,5,24]{2,1,0:T(8,128)S(1)} collective-permute-done((f32[8,5,24]{2,1,0:T(8,128)S(1)}, f32[8,5,24]{2,1,0:T(8,128)S(1)}, u32[]{:S(2)}, u32[]{:S(2)}) %collective-permute-start.2) | collective-permute-done | bytes 3872 | tf_op jit(solution)/shard_map/while/body/eval_jaxpr/ppermute | solution.py:45
  491.6 2.5 fusion.85
  494.8 14.2 %collective-permute-done.2 = f32[8,5,24]{2,1,0:T(8,128)S(1)} collective-permute-done((f32[8,5,24]{2,1,0:T(8,128)S(1)}, f32[8,5,24]{2,1,0:T(8,128)S(1)}, u32[]{:S(2)}, u32[]{:S(2)}) %collective-permute-start.2) | collective-permute-done | bytes 3872 | tf_op jit(solution)/shard_map/while/body/eval_jaxpr/ppermute | solution.py:45
  513.4 2.5 fusion.85
  516.6 14.2 %collective-permute-done.2 = f32[8,5,24]{2,1,0:T(8,128)S(1)} collective-permute-done((f32[8,5,24]{2,1,0:T(8,128)S(1)}, f32[8,5,24]{2,1,0:T(8,128)S(1)}, u32[]{:S(2)}, u32[]{:S(2)}) %collective-permute-start.2) | collective-permute-done | bytes 3872 | tf_op jit(solution)/shard_map/while/body/eval_jaxpr/ppermute | solution.py:45
  535.2 2.5 fusion.85
  538.4 14.2 %collective-permute-done.2 = f32[8,5,24]{2,1,0:T(8,128)S(1)} collective-permute-done((f32[8,5,24]{2,1,0:T(8,128)S(1)}, f32[8,5,24]{2,1,0:T(8,128)S(1)}, u32[]{:S(2)}, u32[]{:S(2)}) %collective-permute-start.2) | collective-permute-done | bytes 3872 | tf_op jit(solution)/shard_map/while/body/eval_jaxpr/ppermute | solution.py:45
  556.9 2.5 fusion.85
  560.2 14.2 %collective-permute-done.2 = f32[8,5,24]{2,1,0:T(8,128)S(1)} collective-permute-done((f32[8,5,24]{2,1,0:T(8,128)S(1)}, f32[8,5,24]{2,1,0:T(8,128)S(1)}, u32[]{:S(2)}, u32[]{:S(2)}) %collective-permute-start.2) | collective-permute-done | bytes 3872 | tf_op jit(solution)/shard_map/while/body/eval_jaxpr/ppermute | solution.py:45
  578.7 2.5 fusion.85
  582.0 14.2 %collective-permute-done.2 = f32[8,5,24]{2,1,0:T(8,128)S(1)} collective-permute-done((f32[8,5,24]{2,1,0:T(8,128)S(1)}, f32[8,5,24]{2,1,0:T(8,128)S(1)}, u32[]{:S(2)}, u32[]{:S(2)}) %collective-permute-start.2) | collective-permute-done | bytes 3872 | tf_op jit(solution)/shard_map/while/body/eval_jaxpr/ppermute | solution.py:45
  600.5 2.5 fusion.85
  603.8 14.2 %collective-permute-done.2 = f32[8,5,24]{2,1,0:T(8,128)S(1)} collective-permute-done((f32[8,5,24]{2,1,0:T(8,128)S(1)}, f32[8,5,24]{2,1,0:T(8,128)S(1)}, u32[]{:S(2)}, u32[]{:S(2)}) %collective-permute-start.2) | collective-permute-done | bytes 3872 | tf_op jit(solution)/shard_map/while/body/eval_jaxpr/ppermute | solution.py:45
  622.3 2.5 fusion.85
  625.6 14.2 %collective-permute-done.2 = f32[8,5,24]{2,1,0:T(8,128)S(1)} collective-permute-done((f32[8,5,24]{2,1,0:T(8,128)S(1)}, f32[8,5,24]{2,1,0:T(8,128)S(1)}, u32[]{:S(2)}, u32[]{:S(2)}) %collective-permute-start.2) | collective-permute-done | bytes 3872 | tf_op jit(solution)/shard_map/while/body/eval_jaxpr/ppermute | solution.py:45
  644.1 2.5 fusion.85
  647.4 14.2 %collective-permute-done.2 = f32[8,5,24]{2,1,0:T(8,128)S(1)} collective-permute-done((f32[8,5,24]{2,1,0:T(8,128)S(1)}, f32[8,5,24]{2,1,0:T(8,128)S(1)}, u32[]{:S(2)}, u32[]{:S(2)}) %collective-permute-start.2) | collective-permute-done | bytes 3872 | tf_op jit(solution)/shard_map/while/body/eval_jaxpr/ppermute | solution.py:45
  669.2 14.2 %collective-permute-done.2 = f32[8,5,24]{2,1,0:T(8,128)S(1)} collective-permute-done((f32[8,5,24]{2,1,0:T(8,128)S(1)}, f32[8,5,24]{2,1,0:T(8,128)S(1)}, u32[]{:S(2)}, u32[]{:S(2)}) %collective-permute-start.2) | collective-permute-done | bytes 3872 | tf_op jit(solution)/shard_map/while/body/eval_jaxpr/ppermute | solution.py:45
  683.7 3.1 bitcast_reduce_fusion.1
  688.5 2.6 fusion.47
  691.8 11.7 %collective-permute-done.5 = f32[8,5,24]{2,1,0:T(8,128)S(1)} collective-permute-done((f32[8,5,24]{2,1,0:T(8,128)S(1)}, f32[8,5,24]{2,1,0:T(8,128)S(1)}, u32[]{:S(2)}, u32[]{:S(2)}) %collective-permute-start.5) | collective-permute-done | bytes 3872 | tf_op jit(solution)/shard_map/ppermute | solution.py:52
  (688 shorter events, 173.2 us)
Async XLA Ops:
  13.8 16.1 %collective-permute-start.1 = (f32[8,5,24,128]{3,2,1,0:T(8,128)S(1)}, f32[8,5,24,128]{3,2,1,0:T(8,128)}, u32[]{:S(2)}, u32[]{:S(2)}) collective-permute-start(f32[8,5,24,128]{3,2,1,0:T(8,128)S(1)} %convolution_add_fusion.3), channel_id=1, source_target_pairs={{0,1},{1,2},{2,3},{3,4},{4,5},{5,6},{6,7},{7,8},{8,9},{9,10},{10,1... | collective-permute-start | bytes 1474568 | tf_op jit(solution)/shard_map/while/body/eval_jaxpr/ppermute | solution.py:45
  13.9 16.0 %collective-permute-start = (bf16[24,40,128]{2,0,1:T(8,128)(2,1)S(1)}, bf16[24,40,128]{2,0,1:T(8,128)(2,1)S(1)}, u32[]{:S(2)}, u32[]{:S(2)}) collective-permute-start(bf16[24,40,128]{2,0,1:T(8,128)(2,1)S(1)} %copy.72), channel_id=1, source_target_pairs={{0,1},{1,2},{2,3},{3,4},{4,5},{5,6},{6,7},{7,8},{8,9},{9,10},{10,1... | collective-permute-start | bytes 737288 | tf_op jit(solution)/shard_map/while/body/eval_jaxpr/ppermute | solution.py:45
  15.2 14.8 %collective-permute-start.3 = (f32[8,5,24]{2,1,0:T(8,128)S(1)}, f32[8,5,24]{2,1,0:T(8,128)S(1)}, u32[]{:S(2)}, u32[]{:S(2)}) collective-permute-start(f32[8,5,24]{2,1,0:T(8,128)S(1)} %get-tuple-element.511), channel_id=1, source_target_pairs={{0,1},{1,2},{2,3},{3,4},{4,5},{5,6},{6,7},{7,8},{8,9},{9,10},{10,1... | collective-permute-start | bytes 11528 | tf_op jit(solution)/shard_map/while/body/eval_jaxpr/ppermute | solution.py:45
  36.7 15.0 %collective-permute-start.1 = (f32[8,5,24,128]{3,2,1,0:T(8,128)S(1)}, f32[8,5,24,128]{3,2,1,0:T(8,128)}, u32[]{:S(2)}, u32[]{:S(2)}) collective-permute-start(f32[8,5,24,128]{3,2,1,0:T(8,128)S(1)} %convolution_add_fusion.3), channel_id=1, source_target_pairs={{0,1},{1,2},{2,3},{3,4},{4,5},{5,6},{6,7},{7,8},{8,9},{9,10},{10,1... | collective-permute-start | bytes 1474568 | tf_op jit(solution)/shard_map/while/body/eval_jaxpr/ppermute | solution.py:45
  36.8 14.9 %collective-permute-start = (bf16[24,40,128]{2,0,1:T(8,128)(2,1)S(1)}, bf16[24,40,128]{2,0,1:T(8,128)(2,1)S(1)}, u32[]{:S(2)}, u32[]{:S(2)}) collective-permute-start(bf16[24,40,128]{2,0,1:T(8,128)(2,1)S(1)} %copy.72), channel_id=1, source_target_pairs={{0,1},{1,2},{2,3},{3,4},{4,5},{5,6},{6,7},{7,8},{8,9},{9,10},{10,1... | collective-permute-start | bytes 737288 | tf_op jit(solution)/shard_map/while/body/eval_jaxpr/ppermute | solution.py:45
  58.5 15.0 %collective-permute-start.1 = (f32[8,5,24,128]{3,2,1,0:T(8,128)S(1)}, f32[8,5,24,128]{3,2,1,0:T(8,128)}, u32[]{:S(2)}, u32[]{:S(2)}) collective-permute-start(f32[8,5,24,128]{3,2,1,0:T(8,128)S(1)} %convolution_add_fusion.3), channel_id=1, source_target_pairs={{0,1},{1,2},{2,3},{3,4},{4,5},{5,6},{6,7},{7,8},{8,9},{9,10},{10,1... | collective-permute-start | bytes 1474568 | tf_op jit(solution)/shard_map/while/body/eval_jaxpr/ppermute | solution.py:45
  58.6 14.9 %collective-permute-start = (bf16[24,40,128]{2,0,1:T(8,128)(2,1)S(1)}, bf16[24,40,128]{2,0,1:T(8,128)(2,1)S(1)}, u32[]{:S(2)}, u32[]{:S(2)}) collective-permute-start(bf16[24,40,128]{2,0,1:T(8,128)(2,1)S(1)} %copy.72), channel_id=1, source_target_pairs={{0,1},{1,2},{2,3},{3,4},{4,5},{5,6},{6,7},{7,8},{8,9},{9,10},{10,1... | collective-permute-start | bytes 737288 | tf_op jit(solution)/shard_map/while/body/eval_jaxpr/ppermute | solution.py:45
  58.8 14.7 %collective-permute-start.3 = (f32[8,5,24]{2,1,0:T(8,128)S(1)}, f32[8,5,24]{2,1,0:T(8,128)S(1)}, u32[]{:S(2)}, u32[]{:S(2)}) collective-permute-start(f32[8,5,24]{2,1,0:T(8,128)S(1)} %get-tuple-element.511), channel_id=1, source_target_pairs={{0,1},{1,2},{2,3},{3,4},{4,5},{5,6},{6,7},{7,8},{8,9},{9,10},{10,1... | collective-permute-start | bytes 11528 | tf_op jit(solution)/shard_map/while/body/eval_jaxpr/ppermute | solution.py:45
  80.3 15.0 %collective-permute-start.1 = (f32[8,5,24,128]{3,2,1,0:T(8,128)S(1)}, f32[8,5,24,128]{3,2,1,0:T(8,128)}, u32[]{:S(2)}, u32[]{:S(2)}) collective-permute-start(f32[8,5,24,128]{3,2,1,0:T(8,128)S(1)} %convolution_add_fusion.3), channel_id=1, source_target_pairs={{0,1},{1,2},{2,3},{3,4},{4,5},{5,6},{6,7},{7,8},{8,9},{9,10},{10,1... | collective-permute-start | bytes 1474568 | tf_op jit(solution)/shard_map/while/body/eval_jaxpr/ppermute | solution.py:45
  80.4 14.9 %collective-permute-start = (bf16[24,40,128]{2,0,1:T(8,128)(2,1)S(1)}, bf16[24,40,128]{2,0,1:T(8,128)(2,1)S(1)}, u32[]{:S(2)}, u32[]{:S(2)}) collective-permute-start(bf16[24,40,128]{2,0,1:T(8,128)(2,1)S(1)} %copy.72), channel_id=1, source_target_pairs={{0,1},{1,2},{2,3},{3,4},{4,5},{5,6},{6,7},{7,8},{8,9},{9,10},{10,1... | collective-permute-start | bytes 737288 | tf_op jit(solution)/shard_map/while/body/eval_jaxpr/ppermute | solution.py:45
  102.1 15.0 %collective-permute-start.1 = (f32[8,5,24,128]{3,2,1,0:T(8,128)S(1)}, f32[8,5,24,128]{3,2,1,0:T(8,128)}, u32[]{:S(2)}, u32[]{:S(2)}) collective-permute-start(f32[8,5,24,128]{3,2,1,0:T(8,128)S(1)} %convolution_add_fusion.3), channel_id=1, source_target_pairs={{0,1},{1,2},{2,3},{3,4},{4,5},{5,6},{6,7},{7,8},{8,9},{9,10},{10,1... | collective-permute-start | bytes 1474568 | tf_op jit(solution)/shard_map/while/body/eval_jaxpr/ppermute | solution.py:45
  102.2 14.9 %collective-permute-start = (bf16[24,40,128]{2,0,1:T(8,128)(2,1)S(1)}, bf16[24,40,128]{2,0,1:T(8,128)(2,1)S(1)}, u32[]{:S(2)}, u32[]{:S(2)}) collective-permute-start(bf16[24,40,128]{2,0,1:T(8,128)(2,1)S(1)} %copy.72), channel_id=1, source_target_pairs={{0,1},{1,2},{2,3},{3,4},{4,5},{5,6},{6,7},{7,8},{8,9},{9,10},{10,1... | collective-permute-start | bytes 737288 | tf_op jit(solution)/shard_map/while/body/eval_jaxpr/ppermute | solution.py:45
  123.9 15.0 %collective-permute-start.1 = (f32[8,5,24,128]{3,2,1,0:T(8,128)S(1)}, f32[8,5,24,128]{3,2,1,0:T(8,128)}, u32[]{:S(2)}, u32[]{:S(2)}) collective-permute-start(f32[8,5,24,128]{3,2,1,0:T(8,128)S(1)} %convolution_add_fusion.3), channel_id=1, source_target_pairs={{0,1},{1,2},{2,3},{3,4},{4,5},{5,6},{6,7},{7,8},{8,9},{9,10},{10,1... | collective-permute-start | bytes 1474568 | tf_op jit(solution)/shard_map/while/body/eval_jaxpr/ppermute | solution.py:45
  124.0 14.9 %collective-permute-start = (bf16[24,40,128]{2,0,1:T(8,128)(2,1)S(1)}, bf16[24,40,128]{2,0,1:T(8,128)(2,1)S(1)}, u32[]{:S(2)}, u32[]{:S(2)}) collective-permute-start(bf16[24,40,128]{2,0,1:T(8,128)(2,1)S(1)} %copy.72), channel_id=1, source_target_pairs={{0,1},{1,2},{2,3},{3,4},{4,5},{5,6},{6,7},{7,8},{8,9},{9,10},{10,1... | collective-permute-start | bytes 737288 | tf_op jit(solution)/shard_map/while/body/eval_jaxpr/ppermute | solution.py:45
  145.7 15.0 %collective-permute-start.1 = (f32[8,5,24,128]{3,2,1,0:T(8,128)S(1)}, f32[8,5,24,128]{3,2,1,0:T(8,128)}, u32[]{:S(2)}, u32[]{:S(2)}) collective-permute-start(f32[8,5,24,128]{3,2,1,0:T(8,128)S(1)} %convolution_add_fusion.3), channel_id=1, source_target_pairs={{0,1},{1,2},{2,3},{3,4},{4,5},{5,6},{6,7},{7,8},{8,9},{9,10},{10,1... | collective-permute-start | bytes 1474568 | tf_op jit(solution)/shard_map/while/body/eval_jaxpr/ppermute | solution.py:45
  145.8 14.9 %collective-permute-start = (bf16[24,40,128]{2,0,1:T(8,128)(2,1)S(1)}, bf16[24,40,128]{2,0,1:T(8,128)(2,1)S(1)}, u32[]{:S(2)}, u32[]{:S(2)}) collective-permute-start(bf16[24,40,128]{2,0,1:T(8,128)(2,1)S(1)} %copy.72), channel_id=1, source_target_pairs={{0,1},{1,2},{2,3},{3,4},{4,5},{5,6},{6,7},{7,8},{8,9},{9,10},{10,1... | collective-permute-start | bytes 737288 | tf_op jit(solution)/shard_map/while/body/eval_jaxpr/ppermute | solution.py:45
  167.5 15.0 %collective-permute-start.1 = (f32[8,5,24,128]{3,2,1,0:T(8,128)S(1)}, f32[8,5,24,128]{3,2,1,0:T(8,128)}, u32[]{:S(2)}, u32[]{:S(2)}) collective-permute-start(f32[8,5,24,128]{3,2,1,0:T(8,128)S(1)} %convolution_add_fusion.3), channel_id=1, source_target_pairs={{0,1},{1,2},{2,3},{3,4},{4,5},{5,6},{6,7},{7,8},{8,9},{9,10},{10,1... | collective-permute-start | bytes 1474568 | tf_op jit(solution)/shard_map/while/body/eval_jaxpr/ppermute | solution.py:45
  167.6 14.9 %collective-permute-start = (bf16[24,40,128]{2,0,1:T(8,128)(2,1)S(1)}, bf16[24,40,128]{2,0,1:T(8,128)(2,1)S(1)}, u32[]{:S(2)}, u32[]{:S(2)}) collective-permute-start(bf16[24,40,128]{2,0,1:T(8,128)(2,1)S(1)} %copy.72), channel_id=1, source_target_pairs={{0,1},{1,2},{2,3},{3,4},{4,5},{5,6},{6,7},{7,8},{8,9},{9,10},{10,1... | collective-permute-start | bytes 737288 | tf_op jit(solution)/shard_map/while/body/eval_jaxpr/ppermute | solution.py:45
  189.3 15.0 %collective-permute-start.1 = (f32[8,5,24,128]{3,2,1,0:T(8,128)S(1)}, f32[8,5,24,128]{3,2,1,0:T(8,128)}, u32[]{:S(2)}, u32[]{:S(2)}) collective-permute-start(f32[8,5,24,128]{3,2,1,0:T(8,128)S(1)} %convolution_add_fusion.3), channel_id=1, source_target_pairs={{0,1},{1,2},{2,3},{3,4},{4,5},{5,6},{6,7},{7,8},{8,9},{9,10},{10,1... | collective-permute-start | bytes 1474568 | tf_op jit(solution)/shard_map/while/body/eval_jaxpr/ppermute | solution.py:45
  189.4 14.9 %collective-permute-start = (bf16[24,40,128]{2,0,1:T(8,128)(2,1)S(1)}, bf16[24,40,128]{2,0,1:T(8,128)(2,1)S(1)}, u32[]{:S(2)}, u32[]{:S(2)}) collective-permute-start(bf16[24,40,128]{2,0,1:T(8,128)(2,1)S(1)} %copy.72), channel_id=1, source_target_pairs={{0,1},{1,2},{2,3},{3,4},{4,5},{5,6},{6,7},{7,8},{8,9},{9,10},{10,1... | collective-permute-start | bytes 737288 | tf_op jit(solution)/shard_map/while/body/eval_jaxpr/ppermute | solution.py:45
  211.1 15.0 %collective-permute-start.1 = (f32[8,5,24,128]{3,2,1,0:T(8,128)S(1)}, f32[8,5,24,128]{3,2,1,0:T(8,128)}, u32[]{:S(2)}, u32[]{:S(2)}) collective-permute-start(f32[8,5,24,128]{3,2,1,0:T(8,128)S(1)} %convolution_add_fusion.3), channel_id=1, source_target_pairs={{0,1},{1,2},{2,3},{3,4},{4,5},{5,6},{6,7},{7,8},{8,9},{9,10},{10,1... | collective-permute-start | bytes 1474568 | tf_op jit(solution)/shard_map/while/body/eval_jaxpr/ppermute | solution.py:45
  211.2 14.9 %collective-permute-start = (bf16[24,40,128]{2,0,1:T(8,128)(2,1)S(1)}, bf16[24,40,128]{2,0,1:T(8,128)(2,1)S(1)}, u32[]{:S(2)}, u32[]{:S(2)}) collective-permute-start(bf16[24,40,128]{2,0,1:T(8,128)(2,1)S(1)} %copy.72), channel_id=1, source_target_pairs={{0,1},{1,2},{2,3},{3,4},{4,5},{5,6},{6,7},{7,8},{8,9},{9,10},{10,1... | collective-permute-start | bytes 737288 | tf_op jit(solution)/shard_map/while/body/eval_jaxpr/ppermute | solution.py:45
  232.9 15.0 %collective-permute-start.1 = (f32[8,5,24,128]{3,2,1,0:T(8,128)S(1)}, f32[8,5,24,128]{3,2,1,0:T(8,128)}, u32[]{:S(2)}, u32[]{:S(2)}) collective-permute-start(f32[8,5,24,128]{3,2,1,0:T(8,128)S(1)} %convolution_add_fusion.3), channel_id=1, source_target_pairs={{0,1},{1,2},{2,3},{3,4},{4,5},{5,6},{6,7},{7,8},{8,9},{9,10},{10,1... | collective-permute-start | bytes 1474568 | tf_op jit(solution)/shard_map/while/body/eval_jaxpr/ppermute | solution.py:45
  233.0 14.9 %collective-permute-start = (bf16[24,40,128]{2,0,1:T(8,128)(2,1)S(1)}, bf16[24,40,128]{2,0,1:T(8,128)(2,1)S(1)}, u32[]{:S(2)}, u32[]{:S(2)}) collective-permute-start(bf16[24,40,128]{2,0,1:T(8,128)(2,1)S(1)} %copy.72), channel_id=1, source_target_pairs={{0,1},{1,2},{2,3},{3,4},{4,5},{5,6},{6,7},{7,8},{8,9},{9,10},{10,1... | collective-permute-start | bytes 737288 | tf_op jit(solution)/shard_map/while/body/eval_jaxpr/ppermute | solution.py:45
  254.6 15.0 %collective-permute-start.1 = (f32[8,5,24,128]{3,2,1,0:T(8,128)S(1)}, f32[8,5,24,128]{3,2,1,0:T(8,128)}, u32[]{:S(2)}, u32[]{:S(2)}) collective-permute-start(f32[8,5,24,128]{3,2,1,0:T(8,128)S(1)} %convolution_add_fusion.3), channel_id=1, source_target_pairs={{0,1},{1,2},{2,3},{3,4},{4,5},{5,6},{6,7},{7,8},{8,9},{9,10},{10,1... | collective-permute-start | bytes 1474568 | tf_op jit(solution)/shard_map/while/body/eval_jaxpr/ppermute | solution.py:45
  254.8 14.9 %collective-permute-start = (bf16[24,40,128]{2,0,1:T(8,128)(2,1)S(1)}, bf16[24,40,128]{2,0,1:T(8,128)(2,1)S(1)}, u32[]{:S(2)}, u32[]{:S(2)}) collective-permute-start(bf16[24,40,128]{2,0,1:T(8,128)(2,1)S(1)} %copy.72), channel_id=1, source_target_pairs={{0,1},{1,2},{2,3},{3,4},{4,5},{5,6},{6,7},{7,8},{8,9},{9,10},{10,1... | collective-permute-start | bytes 737288 | tf_op jit(solution)/shard_map/while/body/eval_jaxpr/ppermute | solution.py:45
  276.4 15.0 %collective-permute-start.1 = (f32[8,5,24,128]{3,2,1,0:T(8,128)S(1)}, f32[8,5,24,128]{3,2,1,0:T(8,128)}, u32[]{:S(2)}, u32[]{:S(2)}) collective-permute-start(f32[8,5,24,128]{3,2,1,0:T(8,128)S(1)} %convolution_add_fusion.3), channel_id=1, source_target_pairs={{0,1},{1,2},{2,3},{3,4},{4,5},{5,6},{6,7},{7,8},{8,9},{9,10},{10,1... | collective-permute-start | bytes 1474568 | tf_op jit(solution)/shard_map/while/body/eval_jaxpr/ppermute | solution.py:45
  276.6 14.9 %collective-permute-start = (bf16[24,40,128]{2,0,1:T(8,128)(2,1)S(1)}, bf16[24,40,128]{2,0,1:T(8,128)(2,1)S(1)}, u32[]{:S(2)}, u32[]{:S(2)}) collective-permute-start(bf16[24,40,128]{2,0,1:T(8,128)(2,1)S(1)} %copy.72), channel_id=1, source_target_pairs={{0,1},{1,2},{2,3},{3,4},{4,5},{5,6},{6,7},{7,8},{8,9},{9,10},{10,1... | collective-permute-start | bytes 737288 | tf_op jit(solution)/shard_map/while/body/eval_jaxpr/ppermute | solution.py:45
  298.2 15.0 %collective-permute-start.1 = (f32[8,5,24,128]{3,2,1,0:T(8,128)S(1)}, f32[8,5,24,128]{3,2,1,0:T(8,128)}, u32[]{:S(2)}, u32[]{:S(2)}) collective-permute-start(f32[8,5,24,128]{3,2,1,0:T(8,128)S(1)} %convolution_add_fusion.3), channel_id=1, source_target_pairs={{0,1},{1,2},{2,3},{3,4},{4,5},{5,6},{6,7},{7,8},{8,9},{9,10},{10,1... | collective-permute-start | bytes 1474568 | tf_op jit(solution)/shard_map/while/body/eval_jaxpr/ppermute | solution.py:45
  298.3 14.9 %collective-permute-start = (bf16[24,40,128]{2,0,1:T(8,128)(2,1)S(1)}, bf16[24,40,128]{2,0,1:T(8,128)(2,1)S(1)}, u32[]{:S(2)}, u32[]{:S(2)}) collective-permute-start(bf16[24,40,128]{2,0,1:T(8,128)(2,1)S(1)} %copy.72), channel_id=1, source_target_pairs={{0,1},{1,2},{2,3},{3,4},{4,5},{5,6},{6,7},{7,8},{8,9},{9,10},{10,1... | collective-permute-start | bytes 737288 | tf_op jit(solution)/shard_map/while/body/eval_jaxpr/ppermute | solution.py:45
  320.0 15.0 %collective-permute-start.1 = (f32[8,5,24,128]{3,2,1,0:T(8,128)S(1)}, f32[8,5,24,128]{3,2,1,0:T(8,128)}, u32[]{:S(2)}, u32[]{:S(2)}) collective-permute-start(f32[8,5,24,128]{3,2,1,0:T(8,128)S(1)} %convolution_add_fusion.3), channel_id=1, source_target_pairs={{0,1},{1,2},{2,3},{3,4},{4,5},{5,6},{6,7},{7,8},{8,9},{9,10},{10,1... | collective-permute-start | bytes 1474568 | tf_op jit(solution)/shard_map/while/body/eval_jaxpr/ppermute | solution.py:45
  320.1 14.9 %collective-permute-start = (bf16[24,40,128]{2,0,1:T(8,128)(2,1)S(1)}, bf16[24,40,128]{2,0,1:T(8,128)(2,1)S(1)}, u32[]{:S(2)}, u32[]{:S(2)}) collective-permute-start(bf16[24,40,128]{2,0,1:T(8,128)(2,1)S(1)} %copy.72), channel_id=1, source_target_pairs={{0,1},{1,2},{2,3},{3,4},{4,5},{5,6},{6,7},{7,8},{8,9},{9,10},{10,1... | collective-permute-start | bytes 737288 | tf_op jit(solution)/shard_map/while/body/eval_jaxpr/ppermute | solution.py:45
  341.8 15.0 %collective-permute-start.1 = (f32[8,5,24,128]{3,2,1,0:T(8,128)S(1)}, f32[8,5,24,128]{3,2,1,0:T(8,128)}, u32[]{:S(2)}, u32[]{:S(2)}) collective-permute-start(f32[8,5,24,128]{3,2,1,0:T(8,128)S(1)} %convolution_add_fusion.3), channel_id=1, source_target_pairs={{0,1},{1,2},{2,3},{3,4},{4,5},{5,6},{6,7},{7,8},{8,9},{9,10},{10,1... | collective-permute-start | bytes 1474568 | tf_op jit(solution)/shard_map/while/body/eval_jaxpr/ppermute | solution.py:45
  341.9 14.9 %collective-permute-start = (bf16[24,40,128]{2,0,1:T(8,128)(2,1)S(1)}, bf16[24,40,128]{2,0,1:T(8,128)(2,1)S(1)}, u32[]{:S(2)}, u32[]{:S(2)}) collective-permute-start(bf16[24,40,128]{2,0,1:T(8,128)(2,1)S(1)} %copy.72), channel_id=1, source_target_pairs={{0,1},{1,2},{2,3},{3,4},{4,5},{5,6},{6,7},{7,8},{8,9},{9,10},{10,1... | collective-permute-start | bytes 737288 | tf_op jit(solution)/shard_map/while/body/eval_jaxpr/ppermute | solution.py:45
  363.6 15.0 %collective-permute-start.1 = (f32[8,5,24,128]{3,2,1,0:T(8,128)S(1)}, f32[8,5,24,128]{3,2,1,0:T(8,128)}, u32[]{:S(2)}, u32[]{:S(2)}) collective-permute-start(f32[8,5,24,128]{3,2,1,0:T(8,128)S(1)} %convolution_add_fusion.3), channel_id=1, source_target_pairs={{0,1},{1,2},{2,3},{3,4},{4,5},{5,6},{6,7},{7,8},{8,9},{9,10},{10,1... | collective-permute-start | bytes 1474568 | tf_op jit(solution)/shard_map/while/body/eval_jaxpr/ppermute | solution.py:45
  363.7 14.9 %collective-permute-start = (bf16[24,40,128]{2,0,1:T(8,128)(2,1)S(1)}, bf16[24,40,128]{2,0,1:T(8,128)(2,1)S(1)}, u32[]{:S(2)}, u32[]{:S(2)}) collective-permute-start(bf16[24,40,128]{2,0,1:T(8,128)(2,1)S(1)} %copy.72), channel_id=1, source_target_pairs={{0,1},{1,2},{2,3},{3,4},{4,5},{5,6},{6,7},{7,8},{8,9},{9,10},{10,1... | collective-permute-start | bytes 737288 | tf_op jit(solution)/shard_map/while/body/eval_jaxpr/ppermute | solution.py:45
  385.4 15.0 %collective-permute-start.1 = (f32[8,5,24,128]{3,2,1,0:T(8,128)S(1)}, f32[8,5,24,128]{3,2,1,0:T(8,128)}, u32[]{:S(2)}, u32[]{:S(2)}) collective-permute-start(f32[8,5,24,128]{3,2,1,0:T(8,128)S(1)} %convolution_add_fusion.3), channel_id=1, source_target_pairs={{0,1},{1,2},{2,3},{3,4},{4,5},{5,6},{6,7},{7,8},{8,9},{9,10},{10,1... | collective-permute-start | bytes 1474568 | tf_op jit(solution)/shard_map/while/body/eval_jaxpr/ppermute | solution.py:45
  385.5 14.9 %collective-permute-start = (bf16[24,40,128]{2,0,1:T(8,128)(2,1)S(1)}, bf16[24,40,128]{2,0,1:T(8,128)(2,1)S(1)}, u32[]{:S(2)}, u32[]{:S(2)}) collective-permute-start(bf16[24,40,128]{2,0,1:T(8,128)(2,1)S(1)} %copy.72), channel_id=1, source_target_pairs={{0,1},{1,2},{2,3},{3,4},{4,5},{5,6},{6,7},{7,8},{8,9},{9,10},{10,1... | collective-permute-start | bytes 737288 | tf_op jit(solution)/shard_map/while/body/eval_jaxpr/ppermute | solution.py:45
  407.2 15.0 %collective-permute-start.1 = (f32[8,5,24,128]{3,2,1,0:T(8,128)S(1)}, f32[8,5,24,128]{3,2,1,0:T(8,128)}, u32[]{:S(2)}, u32[]{:S(2)}) collective-permute-start(f32[8,5,24,128]{3,2,1,0:T(8,128)S(1)} %convolution_add_fusion.3), channel_id=1, source_target_pairs={{0,1},{1,2},{2,3},{3,4},{4,5},{5,6},{6,7},{7,8},{8,9},{9,10},{10,1... | collective-permute-start | bytes 1474568 | tf_op jit(solution)/shard_map/while/body/eval_jaxpr/ppermute | solution.py:45
  407.3 14.9 %collective-permute-start = (bf16[24,40,128]{2,0,1:T(8,128)(2,1)S(1)}, bf16[24,40,128]{2,0,1:T(8,128)(2,1)S(1)}, u32[]{:S(2)}, u32[]{:S(2)}) collective-permute-start(bf16[24,40,128]{2,0,1:T(8,128)(2,1)S(1)} %copy.72), channel_id=1, source_target_pairs={{0,1},{1,2},{2,3},{3,4},{4,5},{5,6},{6,7},{7,8},{8,9},{9,10},{10,1... | collective-permute-start | bytes 737288 | tf_op jit(solution)/shard_map/while/body/eval_jaxpr/ppermute | solution.py:45
  429.0 15.0 %collective-permute-start.1 = (f32[8,5,24,128]{3,2,1,0:T(8,128)S(1)}, f32[8,5,24,128]{3,2,1,0:T(8,128)}, u32[]{:S(2)}, u32[]{:S(2)}) collective-permute-start(f32[8,5,24,128]{3,2,1,0:T(8,128)S(1)} %convolution_add_fusion.3), channel_id=1, source_target_pairs={{0,1},{1,2},{2,3},{3,4},{4,5},{5,6},{6,7},{7,8},{8,9},{9,10},{10,1... | collective-permute-start | bytes 1474568 | tf_op jit(solution)/shard_map/while/body/eval_jaxpr/ppermute | solution.py:45
  429.1 14.9 %collective-permute-start = (bf16[24,40,128]{2,0,1:T(8,128)(2,1)S(1)}, bf16[24,40,128]{2,0,1:T(8,128)(2,1)S(1)}, u32[]{:S(2)}, u32[]{:S(2)}) collective-permute-start(bf16[24,40,128]{2,0,1:T(8,128)(2,1)S(1)} %copy.72), channel_id=1, source_target_pairs={{0,1},{1,2},{2,3},{3,4},{4,5},{5,6},{6,7},{7,8},{8,9},{9,10},{10,1... | collective-permute-start | bytes 737288 | tf_op jit(solution)/shard_map/while/body/eval_jaxpr/ppermute | solution.py:45
  450.8 15.0 %collective-permute-start.1 = (f32[8,5,24,128]{3,2,1,0:T(8,128)S(1)}, f32[8,5,24,128]{3,2,1,0:T(8,128)}, u32[]{:S(2)}, u32[]{:S(2)}) collective-permute-start(f32[8,5,24,128]{3,2,1,0:T(8,128)S(1)} %convolution_add_fusion.3), channel_id=1, source_target_pairs={{0,1},{1,2},{2,3},{3,4},{4,5},{5,6},{6,7},{7,8},{8,9},{9,10},{10,1... | collective-permute-start | bytes 1474568 | tf_op jit(solution)/shard_map/while/body/eval_jaxpr/ppermute | solution.py:45
  450.9 14.9 %collective-permute-start = (bf16[24,40,128]{2,0,1:T(8,128)(2,1)S(1)}, bf16[24,40,128]{2,0,1:T(8,128)(2,1)S(1)}, u32[]{:S(2)}, u32[]{:S(2)}) collective-permute-start(bf16[24,40,128]{2,0,1:T(8,128)(2,1)S(1)} %copy.72), channel_id=1, source_target_pairs={{0,1},{1,2},{2,3},{3,4},{4,5},{5,6},{6,7},{7,8},{8,9},{9,10},{10,1... | collective-permute-start | bytes 737288 | tf_op jit(solution)/shard_map/while/body/eval_jaxpr/ppermute | solution.py:45
  472.6 15.0 %collective-permute-start.1 = (f32[8,5,24,128]{3,2,1,0:T(8,128)S(1)}, f32[8,5,24,128]{3,2,1,0:T(8,128)}, u32[]{:S(2)}, u32[]{:S(2)}) collective-permute-start(f32[8,5,24,128]{3,2,1,0:T(8,128)S(1)} %convolution_add_fusion.3), channel_id=1, source_target_pairs={{0,1},{1,2},{2,3},{3,4},{4,5},{5,6},{6,7},{7,8},{8,9},{9,10},{10,1... | collective-permute-start | bytes 1474568 | tf_op jit(solution)/shard_map/while/body/eval_jaxpr/ppermute | solution.py:45
  472.7 14.9 %collective-permute-start = (bf16[24,40,128]{2,0,1:T(8,128)(2,1)S(1)}, bf16[24,40,128]{2,0,1:T(8,128)(2,1)S(1)}, u32[]{:S(2)}, u32[]{:S(2)}) collective-permute-start(bf16[24,40,128]{2,0,1:T(8,128)(2,1)S(1)} %copy.72), channel_id=1, source_target_pairs={{0,1},{1,2},{2,3},{3,4},{4,5},{5,6},{6,7},{7,8},{8,9},{9,10},{10,1... | collective-permute-start | bytes 737288 | tf_op jit(solution)/shard_map/while/body/eval_jaxpr/ppermute | solution.py:45
  494.4 15.0 %collective-permute-start.1 = (f32[8,5,24,128]{3,2,1,0:T(8,128)S(1)}, f32[8,5,24,128]{3,2,1,0:T(8,128)}, u32[]{:S(2)}, u32[]{:S(2)}) collective-permute-start(f32[8,5,24,128]{3,2,1,0:T(8,128)S(1)} %convolution_add_fusion.3), channel_id=1, source_target_pairs={{0,1},{1,2},{2,3},{3,4},{4,5},{5,6},{6,7},{7,8},{8,9},{9,10},{10,1... | collective-permute-start | bytes 1474568 | tf_op jit(solution)/shard_map/while/body/eval_jaxpr/ppermute | solution.py:45
  494.5 14.9 %collective-permute-start = (bf16[24,40,128]{2,0,1:T(8,128)(2,1)S(1)}, bf16[24,40,128]{2,0,1:T(8,128)(2,1)S(1)}, u32[]{:S(2)}, u32[]{:S(2)}) collective-permute-start(bf16[24,40,128]{2,0,1:T(8,128)(2,1)S(1)} %copy.72), channel_id=1, source_target_pairs={{0,1},{1,2},{2,3},{3,4},{4,5},{5,6},{6,7},{7,8},{8,9},{9,10},{10,1... | collective-permute-start | bytes 737288 | tf_op jit(solution)/shard_map/while/body/eval_jaxpr/ppermute | solution.py:45
  516.2 15.0 %collective-permute-start.1 = (f32[8,5,24,128]{3,2,1,0:T(8,128)S(1)}, f32[8,5,24,128]{3,2,1,0:T(8,128)}, u32[]{:S(2)}, u32[]{:S(2)}) collective-permute-start(f32[8,5,24,128]{3,2,1,0:T(8,128)S(1)} %convolution_add_fusion.3), channel_id=1, source_target_pairs={{0,1},{1,2},{2,3},{3,4},{4,5},{5,6},{6,7},{7,8},{8,9},{9,10},{10,1... | collective-permute-start | bytes 1474568 | tf_op jit(solution)/shard_map/while/body/eval_jaxpr/ppermute | solution.py:45
  516.3 14.9 %collective-permute-start = (bf16[24,40,128]{2,0,1:T(8,128)(2,1)S(1)}, bf16[24,40,128]{2,0,1:T(8,128)(2,1)S(1)}, u32[]{:S(2)}, u32[]{:S(2)}) collective-permute-start(bf16[24,40,128]{2,0,1:T(8,128)(2,1)S(1)} %copy.72), channel_id=1, source_target_pairs={{0,1},{1,2},{2,3},{3,4},{4,5},{5,6},{6,7},{7,8},{8,9},{9,10},{10,1... | collective-permute-start | bytes 737288 | tf_op jit(solution)/shard_map/while/body/eval_jaxpr/ppermute | solution.py:45
  538.0 15.0 %collective-permute-start.1 = (f32[8,5,24,128]{3,2,1,0:T(8,128)S(1)}, f32[8,5,24,128]{3,2,1,0:T(8,128)}, u32[]{:S(2)}, u32[]{:S(2)}) collective-permute-start(f32[8,5,24,128]{3,2,1,0:T(8,128)S(1)} %convolution_add_fusion.3), channel_id=1, source_target_pairs={{0,1},{1,2},{2,3},{3,4},{4,5},{5,6},{6,7},{7,8},{8,9},{9,10},{10,1... | collective-permute-start | bytes 1474568 | tf_op jit(solution)/shard_map/while/body/eval_jaxpr/ppermute | solution.py:45
  538.1 14.9 %collective-permute-start = (bf16[24,40,128]{2,0,1:T(8,128)(2,1)S(1)}, bf16[24,40,128]{2,0,1:T(8,128)(2,1)S(1)}, u32[]{:S(2)}, u32[]{:S(2)}) collective-permute-start(bf16[24,40,128]{2,0,1:T(8,128)(2,1)S(1)} %copy.72), channel_id=1, source_target_pairs={{0,1},{1,2},{2,3},{3,4},{4,5},{5,6},{6,7},{7,8},{8,9},{9,10},{10,1... | collective-permute-start | bytes 737288 | tf_op jit(solution)/shard_map/while/body/eval_jaxpr/ppermute | solution.py:45
  559.8 15.0 %collective-permute-start.1 = (f32[8,5,24,128]{3,2,1,0:T(8,128)S(1)}, f32[8,5,24,128]{3,2,1,0:T(8,128)}, u32[]{:S(2)}, u32[]{:S(2)}) collective-permute-start(f32[8,5,24,128]{3,2,1,0:T(8,128)S(1)} %convolution_add_fusion.3), channel_id=1, source_target_pairs={{0,1},{1,2},{2,3},{3,4},{4,5},{5,6},{6,7},{7,8},{8,9},{9,10},{10,1... | collective-permute-start | bytes 1474568 | tf_op jit(solution)/shard_map/while/body/eval_jaxpr/ppermute | solution.py:45
  559.9 14.9 %collective-permute-start = (bf16[24,40,128]{2,0,1:T(8,128)(2,1)S(1)}, bf16[24,40,128]{2,0,1:T(8,128)(2,1)S(1)}, u32[]{:S(2)}, u32[]{:S(2)}) collective-permute-start(bf16[24,40,128]{2,0,1:T(8,128)(2,1)S(1)} %copy.72), channel_id=1, source_target_pairs={{0,1},{1,2},{2,3},{3,4},{4,5},{5,6},{6,7},{7,8},{8,9},{9,10},{10,1... | collective-permute-start | bytes 737288 | tf_op jit(solution)/shard_map/while/body/eval_jaxpr/ppermute | solution.py:45
  581.6 15.0 %collective-permute-start.1 = (f32[8,5,24,128]{3,2,1,0:T(8,128)S(1)}, f32[8,5,24,128]{3,2,1,0:T(8,128)}, u32[]{:S(2)}, u32[]{:S(2)}) collective-permute-start(f32[8,5,24,128]{3,2,1,0:T(8,128)S(1)} %convolution_add_fusion.3), channel_id=1, source_target_pairs={{0,1},{1,2},{2,3},{3,4},{4,5},{5,6},{6,7},{7,8},{8,9},{9,10},{10,1... | collective-permute-start | bytes 1474568 | tf_op jit(solution)/shard_map/while/body/eval_jaxpr/ppermute | solution.py:45
  581.7 14.9 %collective-permute-start = (bf16[24,40,128]{2,0,1:T(8,128)(2,1)S(1)}, bf16[24,40,128]{2,0,1:T(8,128)(2,1)S(1)}, u32[]{:S(2)}, u32[]{:S(2)}) collective-permute-start(bf16[24,40,128]{2,0,1:T(8,128)(2,1)S(1)} %copy.72), channel_id=1, source_target_pairs={{0,1},{1,2},{2,3},{3,4},{4,5},{5,6},{6,7},{7,8},{8,9},{9,10},{10,1... | collective-permute-start | bytes 737288 | tf_op jit(solution)/shard_map/while/body/eval_jaxpr/ppermute | solution.py:45
  603.3 15.0 %collective-permute-start.1 = (f32[8,5,24,128]{3,2,1,0:T(8,128)S(1)}, f32[8,5,24,128]{3,2,1,0:T(8,128)}, u32[]{:S(2)}, u32[]{:S(2)}) collective-permute-start(f32[8,5,24,128]{3,2,1,0:T(8,128)S(1)} %convolution_add_fusion.3), channel_id=1, source_target_pairs={{0,1},{1,2},{2,3},{3,4},{4,5},{5,6},{6,7},{7,8},{8,9},{9,10},{10,1... | collective-permute-start | bytes 1474568 | tf_op jit(solution)/shard_map/while/body/eval_jaxpr/ppermute | solution.py:45
  603.5 14.9 %collective-permute-start = (bf16[24,40,128]{2,0,1:T(8,128)(2,1)S(1)}, bf16[24,40,128]{2,0,1:T(8,128)(2,1)S(1)}, u32[]{:S(2)}, u32[]{:S(2)}) collective-permute-start(bf16[24,40,128]{2,0,1:T(8,128)(2,1)S(1)} %copy.72), channel_id=1, source_target_pairs={{0,1},{1,2},{2,3},{3,4},{4,5},{5,6},{6,7},{7,8},{8,9},{9,10},{10,1... | collective-permute-start | bytes 737288 | tf_op jit(solution)/shard_map/while/body/eval_jaxpr/ppermute | solution.py:45
  625.1 15.0 %collective-permute-start.1 = (f32[8,5,24,128]{3,2,1,0:T(8,128)S(1)}, f32[8,5,24,128]{3,2,1,0:T(8,128)}, u32[]{:S(2)}, u32[]{:S(2)}) collective-permute-start(f32[8,5,24,128]{3,2,1,0:T(8,128)S(1)} %convolution_add_fusion.3), channel_id=1, source_target_pairs={{0,1},{1,2},{2,3},{3,4},{4,5},{5,6},{6,7},{7,8},{8,9},{9,10},{10,1... | collective-permute-start | bytes 1474568 | tf_op jit(solution)/shard_map/while/body/eval_jaxpr/ppermute | solution.py:45
  625.3 14.9 %collective-permute-start = (bf16[24,40,128]{2,0,1:T(8,128)(2,1)S(1)}, bf16[24,40,128]{2,0,1:T(8,128)(2,1)S(1)}, u32[]{:S(2)}, u32[]{:S(2)}) collective-permute-start(bf16[24,40,128]{2,0,1:T(8,128)(2,1)S(1)} %copy.72), channel_id=1, source_target_pairs={{0,1},{1,2},{2,3},{3,4},{4,5},{5,6},{6,7},{7,8},{8,9},{9,10},{10,1... | collective-permute-start | bytes 737288 | tf_op jit(solution)/shard_map/while/body/eval_jaxpr/ppermute | solution.py:45
  646.9 15.0 %collective-permute-start.1 = (f32[8,5,24,128]{3,2,1,0:T(8,128)S(1)}, f32[8,5,24,128]{3,2,1,0:T(8,128)}, u32[]{:S(2)}, u32[]{:S(2)}) collective-permute-start(f32[8,5,24,128]{3,2,1,0:T(8,128)S(1)} %convolution_add_fusion.3), channel_id=1, source_target_pairs={{0,1},{1,2},{2,3},{3,4},{4,5},{5,6},{6,7},{7,8},{8,9},{9,10},{10,1... | collective-permute-start | bytes 1474568 | tf_op jit(solution)/shard_map/while/body/eval_jaxpr/ppermute | solution.py:45
  647.0 14.9 %collective-permute-start = (bf16[24,40,128]{2,0,1:T(8,128)(2,1)S(1)}, bf16[24,40,128]{2,0,1:T(8,128)(2,1)S(1)}, u32[]{:S(2)}, u32[]{:S(2)}) collective-permute-start(bf16[24,40,128]{2,0,1:T(8,128)(2,1)S(1)} %copy.72), channel_id=1, source_target_pairs={{0,1},{1,2},{2,3},{3,4},{4,5},{5,6},{6,7},{7,8},{8,9},{9,10},{10,1... | collective-permute-start | bytes 737288 | tf_op jit(solution)/shard_map/while/body/eval_jaxpr/ppermute | solution.py:45
  668.7 15.0 %collective-permute-start.1 = (f32[8,5,24,128]{3,2,1,0:T(8,128)S(1)}, f32[8,5,24,128]{3,2,1,0:T(8,128)}, u32[]{:S(2)}, u32[]{:S(2)}) collective-permute-start(f32[8,5,24,128]{3,2,1,0:T(8,128)S(1)} %convolution_add_fusion.3), channel_id=1, source_target_pairs={{0,1},{1,2},{2,3},{3,4},{4,5},{5,6},{6,7},{7,8},{8,9},{9,10},{10,1... | collective-permute-start | bytes 1474568 | tf_op jit(solution)/shard_map/while/body/eval_jaxpr/ppermute | solution.py:45
  668.8 14.9 %collective-permute-start = (bf16[24,40,128]{2,0,1:T(8,128)(2,1)S(1)}, bf16[24,40,128]{2,0,1:T(8,128)(2,1)S(1)}, u32[]{:S(2)}, u32[]{:S(2)}) collective-permute-start(bf16[24,40,128]{2,0,1:T(8,128)(2,1)S(1)} %copy.72), channel_id=1, source_target_pairs={{0,1},{1,2},{2,3},{3,4},{4,5},{5,6},{6,7},{7,8},{8,9},{9,10},{10,1... | collective-permute-start | bytes 737288 | tf_op jit(solution)/shard_map/while/body/eval_jaxpr/ppermute | solution.py:45
  (98 other events, 973.6 us)
where the time goes:
time: 707 us; the launch traced here: 706 us
  waiting for transfers between devices  461 us (65%)
  matrix products  155 us (22%)
  other arithmetic  59.2 us (8%)
  starting transfers between devices  16.1 us (2%)
  local copies, waits for them, and re-layouts  7.86 us (1%)
    ppermute x124, waiting for transfers between devices, one_step(): return lax.ppermute((q_blk, out_acc, row_max, row_sum), 'cp', send_pairs)  449 us
    dot_general x32, matrix products, absorb(): jnp.einsum('kgts,skd->kgtd', e_cache.astype(jnp.bfloat16), value_cache, p...  78.6 us
    dot_general x32, matrix products, absorb(): jnp.einsum('tkgd,skd->kgts', q_grouped, key_cache, preferred_element_type...  48.9 us
    reduce_sum x64, other arithmetic, absorb(): row_sum = row_sum * rescale_by + e_cache.sum(axis=-1) + e_fresh.sum(axis=-1)  35.1 us
    lt x32, other arithmetic, local_attend(): cache_seen = my_rank * cache_len + jnp.arange(cache_len) < prefix_len[0]  20.3 us
    dot_general x32, matrix products, absorb(): jnp.einsum('tkgd,skd->kgts', q_grouped, key_new, preferred_element_type=j...  16.8 us
    ppermute x124, starting transfers between devices, one_step(): return lax.ppermute((q_blk, out_acc, row_max, row_sum), 'cp', send_pairs)  15.8 us
  transfers between devices with their start and end apart: 127, of which 64 were waited for; matrix products, arithmetic and copies ran while one was open for 0% of the time, Pallas kernels for 0%

commit v1 on v0

v1 whole, which is shorter than its diff:
```python
import functools
import math

import jax
import jax.numpy as jnp
from jax import lax
from jax.experimental import pallas as pl
from jax.experimental.pallas import tpu as pltpu
from jax.sharding import PartitionSpec as P

MASK_FILL = -1e30
LOG2E = math.log2(math.e)
LN2 = math.log(2.0)
CHUNK = 256


def solution(mesh):
    groups = mesh.shape['cp']
    tok_spec = P(('dp', 'cp'))

    def kernel(kv_heads, rows, q_ref, k_ref, vt_ref, bias_ref, o_ref, lse_ref, s0, s1, pbuf):
        scale = LOG2E * q_ref.shape[-1] ** -0.5
        keys = k_ref.shape[1]
        cols = 2 * q_ref.shape[2]
        bounds = [(a, min(a + CHUNK, keys)) for a in range(0, keys, CHUNK)]
        tile = pl.program_id(0)
        my_rank = lax.axis_index('cp')

        def scores(h, s_ref):
            q = jnp.concatenate([q_ref[0, h], q_ref[1, h]], axis=0)
            m8 = jnp.full((8, cols), MASK_FILL, jnp.float32)
            yield None
            for a, b in bounds:
                s = lax.dot_general(k_ref[h, a:b, :], q, (((1,), (1,)), ((), ())), preferred_element_type=jnp.float32)
                bias = bias_ref[a:b, :]
                s = s * scale + jnp.concatenate([bias, bias], axis=1)
                if b == keys:
                    n_new = b - a
                    key = my_rank * rows + lax.broadcasted_iota(jnp.int32, (n_new, cols), 0)
                    col = lax.broadcasted_iota(jnp.int32, (n_new, cols), 1)
                    half = (col >= cols // 2).astype(jnp.int32)
                    col = col - half * (cols // 2)
                    tok5 = (2 * tile + half) * rows * 5 + col
                    s = jnp.where(key * 5 <= tok5, s, MASK_FILL)
                s_ref[a:b, :] = s
                m8 = jnp.maximum(m8, jnp.max(s.reshape((b - a) // 8, 8, cols), axis=0))
                yield None
            yield jnp.max(m8, axis=0, keepdims=True)

        def values(h, s_ref, m):
            l8 = jnp.zeros((8, cols), jnp.float32)
            acc = jnp.zeros((vt_ref.shape[1], cols), jnp.float32)
            yield None
            for a, b in bounds:
                p = jnp.exp2(s_ref[a:b, :] - m)
                l8 = l8 + jnp.sum(p.reshape((b - a) // 8, 8, cols), axis=0)
                acc = acc + lax.dot_general(vt_ref[h, :, a:b], p.astype(jnp.bfloat16), (((1,), (0,)), ((), ())), preferred_element_type=jnp.float32)
                yield None
            l = jnp.sum(l8, axis=0, keepdims=True)
            o = (acc / l).astype(jnp.bfloat16)
            half = cols // 2
            o_ref[0, h] = o[:, :half]
            o_ref[1, h] = o[:, half:]
            lse = (m + jnp.log2(l)) * LN2
            lse_ref[0, h:h + 1, :] = lse[:, :half]
            lse_ref[1, h:h + 1, :] = lse[:, half:]
            yield None

        bufs = (s0, s1)
        m = None
        for x in scores(0, bufs[0]):
            m = x
        for h in range(kv_heads):
            ga = values(h, bufs[h % 2], m)
            gb = scores(h + 1, bufs[(h + 1) % 2]) if h + 1 < kv_heads else iter(())
            m2 = None
            done_a = done_b = False
            while not (done_a and done_b):
                try:
                    m2 = next(gb)
                except StopIteration:
                    done_b = True
                try:
                    next(ga)
                except StopIteration:
                    done_a = True
            m = m2

    def local_attend(queries, key_new, value_new, key_cache, value_cache, prefix_len):
        tok, heads, dim = queries.shape
        cache_len, kv_heads = key_cache.shape[:2]
        ratio = heads // kv_heads
        rows = tok * ratio
        rows_pad = 128
        my_rank = lax.axis_index('cp')
        new_pad = -tok % 16
        q = queries.reshape(tok, kv_heads, ratio, dim).transpose(1, 0, 2, 3).reshape(kv_heads, rows, dim)
        q = jnp.pad(q, ((0, 0), (0, rows_pad - rows), (0, 0)))
        q_all = lax.all_gather(q, 'cp')
        k = jnp.concatenate([key_cache, jnp.pad(key_new, ((0, new_pad), (0, 0), (0, 0)))], axis=0).transpose(1, 0, 2)
        vt = jnp.concatenate([value_cache, jnp.pad(value_new, ((0, new_pad), (0, 0), (0, 0)))], axis=0).transpose(1, 2, 0)
        keys = k.shape[1]
        pos = jnp.arange(keys)
        seen = jnp.where(pos < cache_len, my_rank * cache_len + pos < prefix_len[0], pos < cache_len + tok)
        bias = jnp.broadcast_to(jnp.where(seen, 0.0, MASK_FILL).astype(jnp.float32)[:, None], (keys, 128))
        full = lambda a: pl.BlockSpec(a.shape, lambda i: (0,) * a.ndim)
        o_t, lse = pl.pallas_call(
            functools.partial(kernel, kv_heads, tok),
            grid=(groups // 2,),
            in_specs=[pl.BlockSpec((2, kv_heads, rows_pad, dim), lambda i: (i, 0, 0, 0)), full(k), full(vt), full(bias)],
            out_specs=[pl.BlockSpec((2, kv_heads, dim, rows_pad), lambda i: (i, 0, 0, 0)), pl.BlockSpec((2, kv_heads, rows_pad), lambda i: (i, 0, 0))],
            out_shape=[jax.ShapeDtypeStruct((groups, kv_heads, dim, rows_pad), jnp.bfloat16), jax.ShapeDtypeStruct((groups, kv_heads, rows_pad), jnp.float32)],
            scratch_shapes=[pltpu.VMEM((keys, 2 * rows_pad), jnp.float32), pltpu.VMEM((keys, 2 * rows_pad), jnp.float32), pltpu.VMEM((8, 128), jnp.float32)],
            compiler_params=pltpu.CompilerParams(vmem_limit_bytes=60 * 1024 * 1024),
            name='attend',
        )(q_all, k, vt, bias)
        o_all = lax.all_to_all(o_t, 'cp', 0, 0)
        lse_all = lax.all_to_all(lse, 'cp', 0, 0)
        top = jnp.max(lse_all, axis=0)
        w = jnp.exp(lse_all - top)
        w_sum = jnp.sum(w, axis=0)
        out = jnp.sum(o_all.astype(jnp.float32) * w[:, :, None, :], axis=0) / w_sum[:, None, :]
        out = out[:, :, :rows].astype(jnp.bfloat16).reshape(kv_heads, dim, tok, ratio).transpose(2, 0, 3, 1).reshape(tok, heads, dim)
        row_lse = (top + jnp.log(w_sum))[:, :rows].reshape(kv_heads, tok, ratio).transpose(1, 0, 2).reshape(tok, heads)
        return out, row_lse

    return jax.shard_map(local_attend, mesh=mesh, in_specs=(tok_spec, tok_spec, tok_spec, tok_spec, tok_spec, P('dp')), out_specs=(tok_spec, tok_spec), check_vma=False)
```

time: 707 us -> 289 us (0.41)
  the two profiles are of different devices: /device:TPU:96 before, /device:TPU:103 now
where the time goes in v1:
time: 289 us; the launch traced here: 288 us
  waiting for transfers between devices  156 us (54%)
  Pallas kernels  66.3 us (23%)
  local copies, waits for them, and re-layouts  23.5 us (8%)
  between operations  14.8 us (5%)
  blocking collectives  11 us (4%)
  other arithmetic  10.5 us (4%)
  starting transfers between devices  5.63 us (2%)
    all_to_all x1, waiting for transfers between devices, local_attend(): o_all = lax.all_to_all(o_t, 'cp', 0, 0)  112 us
    pallas_call x1, Pallas kernels, local_attend(): pl.pallas_call(functools.partial(kernel, kv_heads, tok), grid=(groups //...  66.3 us
    all_gather x1, waiting for transfers between devices, local_attend(): q_all = lax.all_gather(q, 'cp')  44 us
    all_gather x1, local copies, waits for them, and re-layouts, local_attend(): q_all = lax.all_gather(q, 'cp')  12 us
    all_to_all x1, blocking collectives, local_attend(): lse_all = lax.all_to_all(lse, 'cp', 0, 0)  11 us
    unnamed x9, local copies, waits for them, and re-layouts  9.29 us
  transfers between devices with their start and end apart: 2, of which 2 were waited for; matrix products, arithmetic and copies ran while one was open for 4% of the time, Pallas kernels for 0%

profile of v1, /device:TPU:103, one launch (start us, length us, event | category | flops | bytes accessed | tf_op | source)
XLA Modules:
  0.0 288.0 jit_solution(11139519058262498650)
XLA Ops:
  7.2 0.0 copy-start
  7.2 0.1 all-gather.3.cloned.1.call-start
  7.3 1.1 copy.26
  8.4 0.7 pad.11
  9.2 0.1 all-gather.3.cloned.1.call-update
  9.9 0.8 copy.29
  10.7 1.0 copy.31
  11.7 0.0 copy-done
  11.7 1.7 copy.30
  13.4 3.2 %copy.32 = bf16[1024,8,128]{0,2,1:T(8,128)(2,1)S(1)} copy(bf16[1024,8,128]{2,1,0:T(8,128)(2,1)} %param.10) | data formatting | bytes 4194304 | tf_op args[4]
  16.7 3.1 %fusion.5.k_ref = bf16[8,1056,128]{2,1,0:T(8,128)(2,1)} fusion(bf16[24,8,128]{2,0,1:T(8,128)(2,1)S(1)} %copy.29, bf16[1024,8,128]{2,0,1:T(8,128)(2,1)} %copy.30), kind=kLoop, calls=%fused_computation.8 | loop fusion | flops 6488064 | bytes 4308992 | tf_op jit(solution)/shard_map/transpose | solution.py:100
  19.7 1.7 fusion.3.vt_ref
  21.4 44.0 %all-gather.3.cloned.1.call-done = bf16[256,128,128]{2,0,1:T(8,128)(2,1)} async-done(((bf16[8,128,128]{2,0,1:T(8,128)(2,1)}), bf16[256,128,128]{2,0,1:T(8,128)(2,1)}) %all-gather.3.cloned.1.call-update) | async-done | bytes 8388624 | tf_op jit(solution)/shard_map/all_gather | solution.py:99
  65.4 12.0 %copy.28 = bf16[256,128,128]{2,1,0:T(8,128)(2,1)} copy(bf16[256,128,128]{2,0,1:T(8,128)(2,1)} %all-gather.3.cloned.1.call-done) | data formatting | bytes 16777216 | tf_op jit(solution)/shard_map/all_gather | solution.py:99
  77.4 1.0 broadcast_in_dim.19.bias_ref
  78.4 66.3 %attend.1 = (bf16[32,8,128,128]{3,2,1,0:T(8,128)(2,1)}, f32[32,8,128]{2,1,0:T(8,128)}) custom-call(bf16[32,8,128,128]{3,2,1,0:T(8,128)(2,1)} %bitcast.20, bf16[8,1056,128]{2,1,0:T(8,128)(2,1)} %fusion.5.k_ref, bf16[8,128,1056]{2,1,0:T(8,128)(2,1)} %fusion.3.vt_ref, f32[1056,128]{1,0:T(8,128)} %broadcast_in_dim.19.bias_ref), custom_call_target="tpu_custom_call" | custom-call | tf_op jit(solution)/shard_map/attend/pallas_call | solution.py:107
  144.6 11.0 %all_to_all.10 = f32[32,8,128]{2,1,0:T(8,128)S(1)} all-to-all(f32[32,8,128]{2,1,0:T(8,128)} %get-tuple-element.5), channel_id=1, replica_groups=mesh['dp'=1,'cp'=32] {'cp'}, dimensions={0} | all-to-all | bytes 262144 | tf_op jit(solution)/shard_map/all_to_all | solution.py:118
  155.6 5.6 %all-to-all-start = ((bf16[32,8,128,128]{3,2,1,0:T(8,128)(2,1)}), bf16[32,8,128,128]{3,2,1,0:T(8,128)(2,1)}, u32[]{:S(2)}, u32[]{:S(2)}) async-start(bf16[32,8,128,128]{3,2,1,0:T(8,128)(2,1)} %get-tuple-element.4), calls=%async_computation | async-start | bytes 16777216 | tf_op jit(solution)/shard_map/all_to_all | solution.py:117
  161.3 0.1 reshape.40
  161.4 0.1 copy.35
  161.5 0.7 copy.37
  162.2 112.3 %all-to-all-done = bf16[32,8,128,128]{3,2,1,0:T(8,128)(2,1)} async-done(((bf16[32,8,128,128]{3,2,1,0:T(8,128)(2,1)}), bf16[32,8,128,128]{3,2,1,0:T(8,128)(2,1)}, u32[]{:S(2)}, u32[]{:S(2)}) %all-to-all-start) | async-done | bytes 8388640 | tf_op jit(solution)/shard_map/all_to_all | solution.py:117
  274.5 5.6 %multiply_reduce_fusion = f32[8,128,128]{2,1,0:T(8,128)S(1)} fusion(bf16[32,8,128,128]{3,2,1,0:T(8,128)(2,1)} %all-to-all-done, f32[32,8,128]{2,1,0:T(8,128)S(1)} %get-tuple-element.11), kind=kLoop, calls=%fused_computation | loop fusion | flops 12451840 | bytes 9043968 | tf_op jit(solution)/shard_map/reduce_sum | solution.py:122
  280.1 0.1 fusion.6
  280.2 0.2 copy.33
  280.4 0.7 copy.36
  (7 shorter events, 0.2 us)
Async XLA Ops:
  7.2 4.5 %copy-start = (bf16[1024,8,128]{2,1,0:T(8,128)(2,1)S(1)}, bf16[1024,8,128]{2,1,0:T(8,128)(2,1)}, u32[]{:S(2)}) copy-start(bf16[1024,8,128]{2,1,0:T(8,128)(2,1)} %param.9) | copy-start | bytes 6291460
  7.2 58.2 %all-gather.3.cloned.1.call-start = ((), (), s32[]{:S(2)}) async-start(), calls=%async_computation.2 | async-start | bytes 8650752 | tf_op jit(solution)/shard_map/all_gather | solution.py:99
  155.6 118.9 %all-to-all-start = ((bf16[32,8,128,128]{3,2,1,0:T(8,128)(2,1)}), bf16[32,8,128,128]{3,2,1,0:T(8,128)(2,1)}, u32[]{:S(2)}, u32[]{:S(2)}) async-start(bf16[32,8,128,128]{3,2,1,0:T(8,128)(2,1)} %get-tuple-element.4), calls=%async_computation | async-start | bytes 16777216 | tf_op jit(solution)/shard_map/all_to_all | solution.py:117
Sparse Core Ops, SparseCore 0:
  10.0 55.3 all-gather.2
